TPU v7x, 32 devices: a whole 2x2x4 slice. The times are simulated.
32 devices in a mesh: rep: 8 (over z, core), tp: 4 (over y, x).
Axes of the slice: x: 2, y: 2, z: 4, core: 2. Of those that a mesh axis runs over, the one named last changes fastest.
Arguments:
- delta_query: bfloat16 [8, 2, 2048, 3072], P('rep', None, None, 'tp'), may hold values from -6 to 6
- master_query: float32 [2, 2048, 3072], P(None, 'rep', 'tp'), may hold values from -3 to 3
- moment_query: float32 [2, 2048, 3072], P(None, 'rep', 'tp'), may hold values from -3 to 3
- delta_latent: bfloat16 [8, 2, 512, 4096], P('rep', None, None, 'tp'), may hold values from -6 to 6
- master_latent: float32 [2, 512, 4096], P(None, 'rep', 'tp'), may hold values from -3 to 3
- moment_latent: float32 [2, 512, 4096], P(None, 'rep', 'tp'), may hold values from -3 to 3
- delta_output: bfloat16 [8, 2, 2048, 2048], P('rep', None, 'tp'), may hold values from -6 to 6
- master_output: float32 [2, 2048, 2048], P(None, 'tp', 'rep'), may hold values from -3 to 3
- moment_output: float32 [2, 2048, 2048], P(None, 'tp', 'rep'), may hold values from -3 to 3
Outputs:
- params_query: bfloat16 [2, 2048, 3072], P(None, None, 'tp')
- new_master_query: float32 [2, 2048, 3072], P(None, 'rep', 'tp')
- new_moment_query: float32 [2, 2048, 3072], P(None, 'rep', 'tp')
- params_latent: bfloat16 [2, 512, 4096], P(None, None, 'tp')
- new_master_latent: float32 [2, 512, 4096], P(None, 'rep', 'tp')
- new_moment_latent: float32 [2, 512, 4096], P(None, 'rep', 'tp')
- params_output: bfloat16 [2, 2048, 2048], P(None, 'tp')
- new_master_output: float32 [2, 2048, 2048], P(None, 'tp', 'rep')
- new_moment_output: float32 [2, 2048, 2048], P(None, 'tp', 'rep')
All inputs are finite; a program needn't handle non-finite values.
Results may differ from a plain program's by a relative error of at most 0.012.
Values may be sent and summed in bfloat16 or wider, within the bound.
A program may use at most 128 MiB of HBM per device.

v0:
```python
import jax
import jax.numpy as jnp
from jax import lax
from jax.sharding import PartitionSpec as P

OUTER_RATE = 0.7
OUTER_MOMENTUM = 0.9


def nesterov(totals, master, moment, replica_count):
    average = totals / replica_count
    momentum = OUTER_MOMENTUM * moment + average
    updated = master - OUTER_RATE * (average + OUTER_MOMENTUM * momentum)
    return (updated, momentum)


def outer_step(
    delta_query,
    master_query,
    moment_query,
    delta_latent,
    master_latent,
    moment_latent,
    delta_output,
    master_output,
    moment_output,
):
    replica_count = lax.axis_size("rep")
    query_totals = lax.psum_scatter(
        delta_query[0].astype(jnp.float32).astype(jnp.bfloat16),
        "rep",
        scatter_dimension=1,
        tiled=True,
    ).astype(jnp.float32)
    latent_totals = lax.psum_scatter(
        delta_latent[0].astype(jnp.float32).astype(jnp.bfloat16),
        "rep",
        scatter_dimension=1,
        tiled=True,
    ).astype(jnp.float32)
    output_totals = lax.psum_scatter(
        delta_output[0].astype(jnp.float32).astype(jnp.bfloat16),
        "rep",
        scatter_dimension=2,
        tiled=True,
    ).astype(jnp.float32)
    query_master, query_moment = nesterov(query_totals, master_query, moment_query, replica_count)
    latent_master, latent_moment = nesterov(
        latent_totals, master_latent, moment_latent, replica_count
    )
    output_master, output_moment = nesterov(
        output_totals, master_output, moment_output, replica_count
    )
    query_params = lax.all_gather(query_master.astype(jnp.bfloat16), "rep", axis=1, tiled=True)
    latent_params = lax.all_gather(latent_master.astype(jnp.bfloat16), "rep", axis=1, tiled=True)
    output_params = lax.all_gather(output_master.astype(jnp.bfloat16), "rep", axis=2, tiled=True)
    return (
        query_params,
        query_master,
        query_moment,
        latent_params,
        latent_master,
        latent_moment,
        output_params,
        output_master,
        output_moment,
    )


def on_device(
    delta_query,
    master_query,
    moment_query,
    delta_latent,
    master_latent,
    moment_latent,
    delta_output,
    master_output,
    moment_output,
):
    return outer_step(
        delta_query,
        master_query,
        moment_query,
        delta_latent,
        master_latent,
        moment_latent,
        delta_output,
        master_output,
        moment_output,
    )


def solution(mesh):
    placed = (
        P("rep", None, None, "tp"),
        P(None, "rep", "tp"),
        P(None, "rep", "tp"),
        P("rep", None, None, "tp"),
        P(None, "rep", "tp"),
        P(None, "rep", "tp"),
        P("rep", None, "tp", None),
        P(None, "tp", "rep"),
        P(None, "tp", "rep"),
    )
    return jax.shard_map(
        on_device,
        mesh=mesh,
        in_specs=placed,
        out_specs=(
            P(None, None, "tp"),
            P(None, "rep", "tp"),
            P(None, "rep", "tp"),
            P(None, None, "tp"),
            P(None, "rep", "tp"),
            P(None, "rep", "tp"),
            P(None, "tp", None),
            P(None, "tp", "rep"),
            P(None, "tp", "rep"),
        ),
        check_vma=False,
    )
```

profile of v0, /device:TPU:0, one launch (start us, length us, event | category | flops | bytes accessed | tf_op | source)
XLA Modules:
  0.0 332.2 jit_solution(7297838098868273898)
XLA Ops:
  7.2 0.0 reduce-scatter.6.cloned.1.call-start
  7.2 0.7 reduce-scatter.6.cloned.1.call-update
  7.9 0.0 reduce-scatter.8.cloned.1.call-start
  8.0 0.7 reduce-scatter.8.cloned.1.call-update
  8.7 0.0 reduce-scatter.4.cloned.1.call-start
  8.7 0.7 reduce-scatter.4.cloned.1.call-update
  9.4 0.0 all-gather.6.cloned.1.call-start
  9.4 39.6 %reduce-scatter.6.cloned.1.call-done = bf16[2,64,1024]{2,1,0:T(8,128)(2,1)} async-done(((bf16[2,512,1024]{2,1,0:T(8,128)(2,1)}), bf16[2,64,1024]{2,1,0:T(8,128)(2,1)}) %reduce-scatter.6.cloned.1.call-update) | async-done | bytes 262160 | tf_op jit(solution)/shard_map/reduce_scatter | solution.py:35
  49.1 2.1 fusion.1
  51.2 0.0 all-gather.6.cloned.1.call-update
  51.2 0.0 all-gather.8.cloned.1.call-start
  51.3 48.6 %reduce-scatter.8.cloned.1.call-done = bf16[2,512,256]{2,1,0:T(8,128)(2,1)} async-done(((bf16[2,512,2048]{2,1,0:T(8,128)(2,1)}), bf16[2,512,256]{2,1,0:T(8,128)(2,1)}) %reduce-scatter.8.cloned.1.call-update) | async-done | bytes 524304 | tf_op jit(solution)/shard_map/reduce_scatter | solution.py:41
  99.9 3.6 %fusion = (bf16[2,512,256]{2,1,0:T(8,128)(2,1)}, f32[2,512,256]{2,1,0:T(8,128)}, f32[2,512,256]{2,1,0:T(8,128)}) fusion(f32[2,512,256]{2,1,0:T(8,128)} %param.16, bf16[2,512,256]{2,1,0:T(8,128)(2,1)} %reduce-scatter.8.cloned.1.call-done, f32[2,512,256]{2,1,0:T(8,128)} %param.17), kind=kLoop, calls=%fused_computation.9 | loop fusion | flops 2359296 | bytes 5242880 | tf_op jit(solution)/shard_map/convert_element_type | solution.py:56
  103.5 0.0 all-gather.8.cloned.1.call-update
  103.6 0.0 all-gather.4.cloned.1.call-start
  103.6 66.8 %reduce-scatter.4.cloned.1.call-done = bf16[2,256,768]{2,1,0:T(8,128)(2,1)} async-done(((bf16[2,2048,768]{2,1,0:T(8,128)(2,1)}), bf16[2,256,768]{2,1,0:T(8,128)(2,1)}) %reduce-scatter.4.cloned.1.call-update) | async-done | bytes 786448 | tf_op jit(solution)/shard_map/reduce_scatter | solution.py:29
  170.4 3.5 %fusion.2 = (bf16[2,256,768]{2,1,0:T(8,128)(2,1)}, f32[2,256,768]{2,1,0:T(8,128)}, f32[2,256,768]{2,1,0:T(8,128)}) fusion(f32[2,256,768]{2,1,0:T(8,128)S(1)} %copy-done.2, bf16[2,256,768]{2,1,0:T(8,128)(2,1)} %reduce-scatter.4.cloned.1.call-done, f32[2,256,768]{2,1,0:T(8,128)S(1)} %copy-done.3), kind=kLoop, calls=%fused_computation.11 | loop fusion | flops 3538944 | bytes 7864320 | tf_op jit(solution)/shard_map/convert_element_type | solution.py:54
  174.0 26.2 %all-gather.6.cloned.1.call-done = bf16[2,512,1024]{2,1,0:T(8,128)(2,1)} async-done(((bf16[2,64,1024]{2,1,0:T(8,128)(2,1)}), bf16[2,512,1024]{2,1,0:T(8,128)(2,1)}) %all-gather.6.cloned.1.call-update) | async-done | bytes 2097168 | tf_op jit(solution)/shard_map/all_gather | solution.py:55
  200.1 49.3 %all-gather.8.cloned.1.call-done = bf16[2,512,2048]{2,1,0:T(8,128)(2,1)} async-done(((bf16[2,512,256]{2,1,0:T(8,128)(2,1)}), bf16[2,512,2048]{2,1,0:T(8,128)(2,1)}) %all-gather.8.cloned.1.call-update) | async-done | bytes 4194320 | tf_op jit(solution)/shard_map/all_gather | solution.py:56
  249.4 64.9 %all-gather.4.cloned.1.call-done = bf16[2,2048,768]{2,1,0:T(8,128)(2,1)} async-done(((bf16[2,256,768]{2,1,0:T(8,128)(2,1)}), bf16[2,2048,768]{2,1,0:T(8,128)(2,1)}) %all-gather.4.cloned.1.call-update) | async-done | bytes 6291472 | tf_op jit(solution)/shard_map/all_gather | solution.py:54
  314.3 6.0 %copy.21 = bf16[2,2048,768]{2,1,0:T(8,128)(2,1)} copy(bf16[2,2048,768]{2,1,0:T(8,128)(2,1)} %all-gather.4.cloned.1.call-done) | data formatting | bytes 12582912
  320.4 1.3 copy.22
  321.7 1.6 copy-done
  323.3 2.0 copy.23
  (12 shorter events, 0.0 us)
Async XLA Ops:
  7.2 41.9 %reduce-scatter.6.cloned.1.call-start = ((), (), s32[]{:S(2)}) async-start(), calls=%async_computation.5 | async-start | bytes 2359296 | tf_op jit(solution)/shard_map/reduce_scatter | solution.py:35
  7.9 92.0 %reduce-scatter.8.cloned.1.call-start = ((), (), s32[]{:S(2)}) async-start(), calls=%async_computation.7 | async-start | bytes 4718592 | tf_op jit(solution)/shard_map/reduce_scatter | solution.py:41
  8.7 161.8 %reduce-scatter.4.cloned.1.call-start = ((), (), s32[]{:S(2)}) async-start(), calls=%async_computation.3 | async-start | bytes 7077888 | tf_op jit(solution)/shard_map/reduce_scatter | solution.py:29
  8.7 40.4 %copy-start.4 = (f32[2,64,1024]{2,1,0:T(8,128)S(1)}, f32[2,64,1024]{2,1,0:T(8,128)}, u32[]{:S(2)}) copy-start(f32[2,64,1024]{2,1,0:T(8,128)} %param.13) | copy-start | bytes 1572868
  8.7 40.3 %copy-start.5 = (f32[2,64,1024]{2,1,0:T(8,128)S(1)}, f32[2,64,1024]{2,1,0:T(8,128)}, u32[]{:S(2)}) copy-start(f32[2,64,1024]{2,1,0:T(8,128)} %param.14) | copy-start | bytes 1572868
  9.4 190.7 %all-gather.6.cloned.1.call-start = ((), (), s32[]{:S(2)}) async-start(), calls=%async_computation.6 | async-start | bytes 2359296 | tf_op jit(solution)/shard_map/all_gather | solution.py:55
  51.2 198.2 %all-gather.8.cloned.1.call-start = ((), (), s32[]{:S(2)}) async-start(), calls=%async_computation.8 | async-start | bytes 4718592 | tf_op jit(solution)/shard_map/all_gather | solution.py:56
  99.9 70.5 %copy-start.2 = (f32[2,256,768]{2,1,0:T(8,128)S(1)}, f32[2,256,768]{2,1,0:T(8,128)}, u32[]{:S(2)}) copy-start(f32[2,256,768]{2,1,0:T(8,128)} %param.10) | copy-start | bytes 4718596
  99.9 70.5 %copy-start.3 = (f32[2,256,768]{2,1,0:T(8,128)S(1)}, f32[2,256,768]{2,1,0:T(8,128)}, u32[]{:S(2)}) copy-start(f32[2,256,768]{2,1,0:T(8,128)} %param.11) | copy-start | bytes 4718596
  103.6 210.8 %all-gather.4.cloned.1.call-start = ((), (), s32[]{:S(2)}) async-start(), calls=%async_computation.4 | async-start | bytes 7077888 | tf_op jit(solution)/shard_map/all_gather | solution.py:54
  314.3 6.0 %copy-start.1 = (bf16[2,512,1024]{2,1,0:T(8,128)(2,1)S(1)}, bf16[2,512,1024]{2,1,0:T(8,128)(2,1)}, u32[]{:S(2)}) copy-start(bf16[2,512,1024]{2,1,0:T(8,128)(2,1)} %all-gather.6.cloned.1.call-done) | copy-start | bytes 6291460
  320.4 2.9 copy-start
Sparse Core Ops, SparseCore 0:
  10.3 38.7 reduce-scatter.5
  51.3 48.5 reduce-scatter.7
  102.2 68.1 reduce-scatter.3
  172.5 27.6 all-gather.5
  202.1 47.1 all-gather.7
  251.4 62.8 all-gather.3
where the time goes:
time: 332 us
  waiting for transfers between devices  298 us (90%)
  between operations  14.1 us (4%)
  local copies, waits for them, and re-layouts  11 us (3%)
  other arithmetic  9.27 us (3%)
    reduce_scatter x1, waiting for transfers between devices, outer_step(): lax.psum_scatter(delta_query[0].astype(jnp.float32).astype(jnp.bfloat16),...  66.8 us
    all_gather x1, waiting for transfers between devices, outer_step(): lax.all_gather(query_master.astype(jnp.bfloat16), 'rep', axis=1, tiled=True)  64.9 us
    all_gather x1, waiting for transfers between devices, outer_step(): lax.all_gather(output_master.astype(jnp.bfloat16), 'rep', axis=2, tiled=T...  49.3 us
    reduce_scatter x1, waiting for transfers between devices, outer_step(): lax.psum_scatter(delta_output[0].astype(jnp.float32).astype(jnp.bfloat16)...  48.6 us
    reduce_scatter x1, waiting for transfers between devices, outer_step(): lax.psum_scatter(delta_latent[0].astype(jnp.float32).astype(jnp.bfloat16)...  39.6 us
    all_gather x1, waiting for transfers between devices, outer_step(): lax.all_gather(latent_master.astype(jnp.bfloat16), 'rep', axis=1, tiled=T...  26.2 us
    unnamed x15, local copies, waits for them, and re-layouts  11 us
  transfers between devices with their start and end apart: 6, of which 6 were waited for; matrix products, arithmetic and copies ran while one was open for 3% of the time, Pallas kernels for 0%

commit v1 on v0

--- a/solution.py
+++ b/solution.py
@@ -51,7 +51,11 @@
     output_master, output_moment = nesterov(
         output_totals, master_output, moment_output, replica_count
     )
-    query_params = lax.all_gather(query_master.astype(jnp.bfloat16), "rep", axis=1, tiled=True)
+    x = query_master.astype(jnp.bfloat16)
+    size = lax.axis_size("rep")
+    tiles = jnp.stack([x for _ in range(size)])
+    tiles = lax.all_to_all(tiles, "rep", split_axis=0, concat_axis=0)
+    query_params = jnp.concatenate(tiles, axis=1)
     latent_params = lax.all_gather(latent_master.astype(jnp.bfloat16), "rep", axis=1, tiled=True)
     output_params = lax.all_gather(output_master.astype(jnp.bfloat16), "rep", axis=2, tiled=True)
     return (

time: 332 us -> 379 us (1.14)
  waiting for transfers between devices: 298 us -> 337 us
  starting transfers between devices: 0.24 us -> 5.08 us
    all_gather x1 -> x0, waiting for transfers between devices: 64.9 us -> none  [outer_step(): lax.all_gather(query_master.astype(jnp.bfloat16), 'rep', axis=1, tiled=True)]
    all_gather x1, waiting for transfers between devices: 26.2 us -> 82.3 us  [outer_step(): lax.all_gather(latent_master.astype(jnp.bfloat16), 'rep', axis=1, tiled=T...]
    reduce_scatter x1, waiting for transfers between devices: 48.6 us -> 95.7 us  [outer_step(): lax.psum_scatter(delta_output[0].astype(jnp.float32).astype(jnp.bfloat16)...]
    all_to_all x0 -> x1, local copies, waits for them, and re-layouts: none -> 6.04 us  [outer_step(): tiles = lax.all_to_all(tiles, 'rep', split_axis=0, concat_axis=0)]
    unnamed x15 -> x14, local copies, waits for them, and re-layouts: 11 us -> 4.98 us
    all_to_all x0 -> x1, starting transfers between devices: none -> 4.89 us  [outer_step(): tiles = lax.all_to_all(tiles, 'rep', split_axis=0, concat_axis=0)]
  transfers between devices with their start and end apart: 6 -> 6, of which waited for: 6 -> 5; matrix products, arithmetic and copies ran while one was open for 3% -> 3% of each run, Pallas kernels for 0% -> 0%
where the time goes in v1:
time: 379 us; the launch traced here: 378 us
  waiting for transfers between devices  337 us (89%)
  local copies, waits for them, and re-layouts  14.3 us (4%)
  between operations  13.8 us (4%)
  other arithmetic  8.58 us (2%)
  starting transfers between devices  5.08 us (1%)
    reduce_scatter x1, waiting for transfers between devices, outer_step(): lax.psum_scatter(delta_output[0].astype(jnp.float32).astype(jnp.bfloat16)...  95.7 us
    all_gather x1, waiting for transfers between devices, outer_step(): lax.all_gather(latent_master.astype(jnp.bfloat16), 'rep', axis=1, tiled=T...  82.3 us
    reduce_scatter x1, waiting for transfers between devices, outer_step(): lax.psum_scatter(delta_query[0].astype(jnp.float32).astype(jnp.bfloat16),...  68.1 us
    all_gather x1, waiting for transfers between devices, outer_step(): lax.all_gather(output_master.astype(jnp.bfloat16), 'rep', axis=2, tiled=T...  48.7 us
    reduce_scatter x1, waiting for transfers between devices, outer_step(): lax.psum_scatter(delta_latent[0].astype(jnp.float32).astype(jnp.bfloat16)...  39.6 us
  transfers between devices with their start and end apart: 6, of which 5 were waited for; matrix products, arithmetic and copies ran while one was open for 3% of the time, Pallas kernels for 0%

profile of v1, /device:TPU:0, one launch (start us, length us, event | category | flops | bytes accessed | tf_op | source)
XLA Modules:
  0.0 378.4 jit_solution(7937190650873301014)
XLA Ops:
  7.2 0.0 reduce-scatter.6.cloned.1.call-start
  7.2 0.7 reduce-scatter.6.cloned.1.call-update
  7.9 0.0 reduce-scatter.4.cloned.1.call-start
  8.0 0.7 reduce-scatter.4.cloned.1.call-update
  8.7 0.0 reduce-scatter.8.cloned.1.call-start
  8.7 0.7 reduce-scatter.8.cloned.1.call-update
  9.4 0.0 all-gather.3.cloned.1.call-start
  9.5 39.6 %reduce-scatter.6.cloned.1.call-done = bf16[2,64,1024]{2,1,0:T(8,128)(2,1)} async-done(((bf16[2,512,1024]{2,1,0:T(8,128)(2,1)}), bf16[2,64,1024]{2,1,0:T(8,128)(2,1)}) %reduce-scatter.6.cloned.1.call-update) | async-done | bytes 262160 | tf_op jit(solution)/shard_map/reduce_scatter | solution.py:35
  49.1 2.5 fusion.1
  51.6 0.0 all-gather.3.cloned.1.call-update
  51.6 68.1 %reduce-scatter.4.cloned.1.call-done = bf16[2,256,768]{2,1,0:T(8,128)(2,1)} async-done(((bf16[2,2048,768]{2,1,0:T(8,128)(2,1)}), bf16[2,256,768]{2,1,0:T(8,128)(2,1)}) %reduce-scatter.4.cloned.1.call-update) | async-done | bytes 786448 | tf_op jit(solution)/shard_map/reduce_scatter | solution.py:29
  119.7 3.2 fusion.2
  123.0 3.3 stack.2
  126.3 4.9 %all-to-all-start = ((bf16[8,2,256,768]{3,2,1,0:T(8,128)(2,1)}), bf16[8,2,256,768]{3,2,1,0:T(8,128)(2,1)}, u32[]{:S(2)}, u32[]{:S(2)}) async-start(bf16[8,2,256,768]{3,2,1,0:T(8,128)(2,1)} %stack.2), calls=%async_computation.1 | async-start | bytes 12582912 | tf_op jit(solution)/shard_map/all_to_all | solution.py:57
  131.2 0.0 all-gather.5.cloned.1.call-start
  131.2 95.7 %reduce-scatter.8.cloned.1.call-done = bf16[2,512,256]{2,1,0:T(8,128)(2,1)} async-done(((bf16[2,512,2048]{2,1,0:T(8,128)(2,1)}), bf16[2,512,256]{2,1,0:T(8,128)(2,1)}) %reduce-scatter.8.cloned.1.call-update) | async-done | bytes 524304 | tf_op jit(solution)/shard_map/reduce_scatter | solution.py:41
  227.0 2.8 fusion
  229.8 0.0 all-gather.5.cloned.1.call-update
  229.8 82.3 %all-gather.3.cloned.1.call-done = bf16[2,512,1024]{2,1,0:T(8,128)(2,1)} async-done(((bf16[2,64,1024]{2,1,0:T(8,128)(2,1)}), bf16[2,512,1024]{2,1,0:T(8,128)(2,1)}) %all-gather.3.cloned.1.call-update) | async-done | bytes 2097168 | tf_op jit(solution)/shard_map/all_gather | solution.py:59
  312.1 48.7 %all-gather.5.cloned.1.call-done = bf16[2,512,2048]{2,1,0:T(8,128)(2,1)} async-done(((bf16[2,512,256]{2,1,0:T(8,128)(2,1)}), bf16[2,512,2048]{2,1,0:T(8,128)(2,1)}) %all-gather.5.cloned.1.call-update) | async-done | bytes 4194320 | tf_op jit(solution)/shard_map/all_gather | solution.py:60
  360.8 6.0 %copy.18 = bf16[8,2,256,768]{3,2,0,1:T(8,128)(2,1)} copy(bf16[8,2,256,768]{3,2,1,0:T(8,128)(2,1)} %all-to-all-done) | data formatting | bytes 12582912 | tf_op jit(solution)/shard_map/all_to_all | solution.py:57
  366.9 1.3 copy.21
  368.2 1.6 copy-done
  369.8 2.0 copy.22
  (12 shorter events, 0.0 us)
Async XLA Ops:
  7.2 41.9 %reduce-scatter.6.cloned.1.call-start = ((), (), s32[]{:S(2)}) async-start(), calls=%async_computation.5 | async-start | bytes 2359296 | tf_op jit(solution)/shard_map/reduce_scatter | solution.py:35
  7.9 111.8 %reduce-scatter.4.cloned.1.call-start = ((), (), s32[]{:S(2)}) async-start(), calls=%async_computation.4 | async-start | bytes 7077888 | tf_op jit(solution)/shard_map/reduce_scatter | solution.py:29
  8.7 218.3 %reduce-scatter.8.cloned.1.call-start = ((), (), s32[]{:S(2)}) async-start(), calls=%async_computation.7 | async-start | bytes 4718592 | tf_op jit(solution)/shard_map/reduce_scatter | solution.py:41
  8.7 111.0 %copy-start.3 = (f32[2,256,768]{2,1,0:T(8,128)S(1)}, f32[2,256,768]{2,1,0:T(8,128)}, u32[]{:S(2)}) copy-start(f32[2,256,768]{2,1,0:T(8,128)} %param.11) | copy-start | bytes 4718596
  9.4 110.3 %copy-start.2 = (f32[2,256,768]{2,1,0:T(8,128)S(1)}, f32[2,256,768]{2,1,0:T(8,128)}, u32[]{:S(2)}) copy-start(f32[2,256,768]{2,1,0:T(8,128)} %param.10) | copy-start | bytes 4718596
  9.4 302.7 %all-gather.3.cloned.1.call-start = ((), (), s32[]{:S(2)}) async-start(), calls=%async_computation.6 | async-start | bytes 2359296 | tf_op jit(solution)/shard_map/all_gather | solution.py:59
  126.3 100.7 %copy-start.4 = (f32[2,512,256]{2,1,0:T(8,128)S(1)}, f32[2,512,256]{2,1,0:T(8,128)}, u32[]{:S(2)}) copy-start(f32[2,512,256]{2,1,0:T(8,128)} %param.16) | copy-start | bytes 3145732
  126.3 100.7 %copy-start.5 = (f32[2,512,256]{2,1,0:T(8,128)S(1)}, f32[2,512,256]{2,1,0:T(8,128)}, u32[]{:S(2)}) copy-start(f32[2,512,256]{2,1,0:T(8,128)} %param.17) | copy-start | bytes 3145732
  126.3 234.5 %all-to-all-start = ((bf16[8,2,256,768]{3,2,1,0:T(8,128)(2,1)}), bf16[8,2,256,768]{3,2,1,0:T(8,128)(2,1)}, u32[]{:S(2)}, u32[]{:S(2)}) async-start(bf16[8,2,256,768]{3,2,1,0:T(8,128)(2,1)} %stack.2), calls=%async_computation.1 | async-start | bytes 12582912 | tf_op jit(solution)/shard_map/all_to_all | solution.py:57
  131.2 229.6 %all-gather.5.cloned.1.call-start = ((), (), s32[]{:S(2)}) async-start(), calls=%async_computation.8 | async-start | bytes 4718592 | tf_op jit(solution)/shard_map/all_gather | solution.py:60
  312.1 54.8 %copy-start.1 = (bf16[2,512,1024]{2,1,0:T(8,128)(2,1)S(1)}, bf16[2,512,1024]{2,1,0:T(8,128)(2,1)}, u32[]{:S(2)}) copy-start(bf16[2,512,1024]{2,1,0:T(8,128)(2,1)} %all-gather.3.cloned.1.call-done) | copy-start | bytes 6291460
  366.9 2.9 copy-start
Sparse Core Ops, SparseCore 0:
  10.3 38.7 reduce-scatter.5
  51.4 68.3 reduce-scatter.3
  122.0 104.9 reduce-scatter.7
  229.0 83.0 all-gather.2
  314.1 46.6 all-gather.4
